TPU v7x, 32 devices: a whole 2x2x4 slice. The times are simulated.
32 devices in a mesh: patch: 8 (over y, x, core), rhs: 4 (over z).
Axes of the slice: x: 2, y: 2, z: 4, core: 2. Of those that a mesh axis runs over, the one named last changes fastest.
Arguments:
- rhs_vectors: float32 [64, 16, 384], P('patch', 'rhs'), may hold values from -8 to 8
- near_blocks: bfloat16 [64, 4, 384, 384], P('patch'), may hold values from -1 to 5, as said below
- neighbours: int32 [64, 4], P('patch'), may hold values from 0 to 63, as said below
- up_maps: float32 [64, 64, 384], P('patch'), may hold values from -0.3125 to 0.3125
- shift_up: float32 [64, 64, 64], P('patch'), may hold values from -0.25 to 0.25
- far_lists: int32 [8, 4], P('patch'), may hold values from 0 to 7, as said below
- translations: float32 [8, 4, 64, 64], P('patch'), may hold values from -0.375 to 0.375
- shift_down: float32 [64, 64, 64], P('patch'), may hold values from -0.75 to 0.75
- down_maps: float32 [64, 384, 64], P('patch'), may hold values from -0.375 to 0.375
Outputs:
- solution: float32 [64, 16, 384], P('patch', 'rhs')
- residual: float32 [64, 16, 384], P('patch', 'rhs')
Inputs may be any that keep to these rules, and one draw needn't show every extreme that they name: `neighbours`: entry 0 of each row is the patch itself; every other entry names a patch of the same cell or of the cell just before or just after it, cyclically. `far_lists`: entry 0 of each row names the cell just before or just after the row's own cell, cyclically, and for cell 0 the cell just before it; every other entry names a cell other than the row's own. `near_blocks`: the blocks keep the operator's symmetric part positive definite.
All inputs are finite; a program needn't handle non-finite values.
Results may differ from a plain program's by a relative error of at most 0.008.
The roundings to bfloat16 on the way count: a program that leaves them out, or rounds other values in their place, can miss the bound.
Values may be sent and summed in bfloat16 or wider, within the bound.
A program may use at most 64 MiB of HBM per device.

v0:
```python
import jax
import jax.numpy as jnp
from jax import lax
from jax.sharding import PartitionSpec as P

ITERS = 2
HIGH = lax.Precision.HIGHEST


def with_halo(block, sides, width):
    for axis, dim in sides:
        count = lax.axis_size(axis)
        forward = [(i, i + 1) for i in range(count - 1)]
        forward.append((count - 1, 0))
        backward = [(target, source) for source, target in forward]
        low = lax.ppermute(
            lax.slice_in_dim(block, block.shape[dim] - width, None, axis=dim), axis, forward
        )
        high = lax.ppermute(lax.slice_in_dim(block, 0, width, axis=dim), axis, backward)
        block = jnp.concatenate([low, block, high], axis=dim)
    return block


def spd_solve(matrix, right):
    factor = jnp.linalg.cholesky(matrix)
    return jax.scipy.linalg.cho_solve((factor, True), right)


def gram(left, right):
    return jnp.einsum("pkw,plw->kl", left, right, precision=HIGH)


def mix(field, coeffs):
    return jnp.einsum("pkw,kl->plw", field, coeffs, precision=HIGH)


def residual_sum(residual):
    return lax.psum(gram(residual, residual), "patch")


def apply_operator(
    field,
    near_blocks,
    neighbours,
    up_maps,
    shift_up,
    far_lists,
    translations,
    shift_down,
    down_maps,
):
    patches = field.shape[0]
    count = lax.axis_size("patch")
    first = lax.axis_index("patch") * patches - patches
    rounded = field.astype(jnp.bfloat16)
    widened = with_halo(rounded, (("patch", 0),), patches)
    local_ids = jnp.mod(neighbours - first, patches * count)
    picked = widened[local_ids]
    near = jnp.einsum("pjvw,pjkw->pkv", near_blocks, picked, preferred_element_type=jnp.float32)
    moments = jnp.einsum("pew,pkw->pke", up_maps, field, precision=HIGH)
    cell_moment = jnp.einsum("pfe,pke->kf", shift_up, moments, precision=HIGH)
    sources = far_lists[0]
    table = translations[0]
    piece = lax.all_gather(cell_moment[None], "patch", axis=0, tiled=True)
    labels = jnp.arange(piece.shape[0], dtype=jnp.int32)
    select = (sources[:, None] == labels[None, :]).astype(jnp.float32)
    chosen = jnp.einsum("ji,ike->jke", select, piece, precision=HIGH)
    local_exp = jnp.zeros_like(cell_moment) + jnp.einsum(
        "jfe,jke->kf", table, chosen, precision=HIGH
    )
    patch_exp = jnp.einsum("pfe,ke->pkf", shift_down, local_exp, precision=HIGH)
    far = jnp.einsum("pvf,pkf->pkv", down_maps, patch_exp, precision=HIGH)
    return near + far


def on_device(
    rhs_vectors,
    near_blocks,
    neighbours,
    up_maps,
    shift_up,
    far_lists,
    translations,
    shift_down,
    down_maps,
):
    my_cols = rhs_vectors.shape[1]
    offset = lax.axis_index("rhs") * my_cols
    residual = lax.all_gather(rhs_vectors, "rhs", axis=1, tiled=True)
    solution = jnp.zeros_like(residual)
    direction = residual
    current = jnp.zeros((residual.shape[1], residual.shape[1]), jnp.float32)
    for step in range(ITERS):
        image = apply_operator(
            direction,
            near_blocks,
            neighbours,
            up_maps,
            shift_up,
            far_lists,
            translations,
            shift_down,
            down_maps,
        )
        if step == 0:
            current = residual_sum(residual)
        curve = lax.psum(gram(direction, image), "patch")
        curve = 0.5 * (curve + curve.T)
        alpha = spd_solve(curve, current)
        solution = solution + mix(direction, alpha)
        residual = residual - mix(image, alpha)
        if step + 1 < ITERS:
            following = residual_sum(residual)
            beta = spd_solve(current, following)
            direction = residual + mix(direction, beta)
            current = following
    solution_mine = lax.dynamic_slice_in_dim(solution, offset, my_cols, 1)
    residual_mine = lax.dynamic_slice_in_dim(residual, offset, my_cols, 1)
    return (solution_mine, residual_mine)


def solution(mesh):
    return jax.shard_map(
        on_device,
        mesh=mesh,
        in_specs=(
            P("patch", "rhs", None),
            P("patch", None, None, None),
            P("patch", None),
            P("patch", None, None),
            P("patch", None, None),
            P("patch", None),
            P("patch", None, None, None),
            P("patch", None, None),
            P("patch", None, None),
        ),
        out_specs=(P("patch", "rhs", None), P("patch", "rhs", None)),
        check_vma=False,
    )
```

profile of v0, /device:TPU:0, one launch (start us, length us, event | category | flops | bytes accessed | tf_op | source)
XLA Modules:
  0.0 129.5 jit_solution(5300560113778208520)
XLA Ops:
  0.6 0.9 copy.61
  1.5 15.5 %all_gather.9 = f32[8,16,384]{2,0,1:T(8,128)S(1)} all-gather(f32[8,4,384]{2,0,1:T(8,128)S(1)} %copy.61), channel_id=1, replica_groups=mesh['patch'=8,'rhs'=4] {'rhs'}, dimensions={1}, use_global_device_ids=true | all-gather | bytes 245760 | tf_op jit(solution)/shard_map/all_gather | solution.py:89
  17.9 0.7 compare_select_fusion
  18.8 2.1 %fusion.11 = f32[8,16,64]{2,1,0:T(8,128)S(1)} fusion(f32[8,64,384]{2,1,0:T(8,128)} %param.15, f32[8,16,384]{2,0,1:T(8,128)S(1)} %all_gather.9), kind=kOutput, calls=%fused_computation.33 | convolution fusion | flops 37748736 | bytes 1015808 | tf_op jit(solution)/shard_map/pew,pkw->pke/dot_general | solution.py:60
  20.9 1.2 convolution_bitcast_fusion.11
  22.1 9.3 %all-gather = f32[128,64]{1,0:T(8,128)S(1)} all-gather(f32[16,64]{1,0:T(8,128)S(1)} %convolution_bitcast_fusion.11), channel_id=2, replica_groups=mesh['patch'=8,'rhs'=4] {'patch'}, dimensions={0}, use_global_device_ids=true | all-gather | bytes 36864 | tf_op jit(solution)/shard_map/all_gather | solution.py:64
  31.4 0.9 fusion.15
  32.3 1.1 fusion.4
  33.4 1.7 %convolution_bitcast_fusion.6 = f32[8,16,64]{2,1,0:T(8,128)S(1)} fusion(f32[16,64,1]{1,0,2:T(8,128)S(1)} %fusion.4, f32[8,64,64]{2,1,0:T(8,128)} %param.19), kind=kOutput, calls=%fused_computation.12 | convolution fusion | flops 6291456 | bytes 167936 | tf_op jit(solution)/shard_map/pfe,ke->pkf/dot_general | solution.py:71
  35.9 6.3 %convolution_bitcast_fusion.4 = f32[8,16,384]{2,1,0:T(8,128)S(1)} fusion(bf16[8,4,16,384]{3,2,1,0:T(8,128)(2,1)S(1)} %bitcast.140, bf16[8,4,384,384]{3,2,1,0:T(8,128)(2,1)} %param.13), kind=kOutput, calls=%fused_computation.10 | convolution fusion | flops 150994944 | bytes 10027008 | tf_op jit(solution)/shard_map/pjvw,pjkw->pkv/dot_general | solution.py:59
  43.2 23.6 %all-reduce = (f32[16,16]{0,1:T(8,128)S(1)}, f32[16,16]{1,0:T(8,128)S(1)}) all-reduce(f32[16,16]{0,1:T(8,128)S(1)} %convolution_bitcast_fusion.14, f32[16,16]{1,0:T(8,128)S(1)} %convolution_bitcast_fusion.15), channel_id=1, replica_groups=mesh['patch'=8,'rhs'=4] {'patch'}, use_global_device_ids=true, to_apply=%region_3.5 | all-reduce | flops 512 | bytes 4096 | tf_op jit(solution)/shard_map/psum | solution.py:38
  67.0 1.5 %cholesky.59 = f32[16,16]{1,0:T(8,128)S(1)} custom-call(f32[16,16]{1,0:T(8,128)S(1)} %fusion.35), custom_call_target="Cholesky" | custom-call | tf_op jit(solution)/shard_map/jit(cholesky)/cholesky | solution.py:25
  69.1 0.6 fusion.20
  69.8 1.2 custom-call.9
  72.1 12.1 %psum.30 = f32[16,16]{1,0:T(8,128)S(1)} all-reduce(f32[16,16]{1,0:T(8,128)S(1)} %convolution_bitcast_fusion.13), channel_id=1, replica_groups=mesh['patch'=8,'rhs'=4] {'patch'}, use_global_device_ids=true, to_apply=%region_4.7 | all-reduce | flops 256 | bytes 2048 | tf_op jit(solution)/shard_map/psum | solution.py:38
  84.2 1.4 %cholesky.70 = f32[16,16]{1,0:T(8,128)S(1)} custom-call(f32[16,16]{1,0:T(8,128)S(1)} %fusion.31), custom_call_target="Cholesky" | custom-call | tf_op jit(solution)/shard_map/jit(cholesky)/cholesky | solution.py:25
  87.0 1.2 custom-call.10
  89.8 0.9 fusion.44
  91.1 9.4 %all-gather.1 = f32[128,64]{1,0:T(8,128)S(1)} all-gather(f32[16,64]{1,0:T(8,128)S(1)} %convolution_bitcast_fusion.8), channel_id=3, replica_groups=mesh['patch'=8,'rhs'=4] {'patch'}, dimensions={0}, use_global_device_ids=true | all-gather | bytes 36864 | tf_op jit(solution)/shard_map/all_gather | solution.py:64
  100.9 0.7 convolution_bitcast_fusion.5
  102.3 6.2 %convolution_bitcast_fusion.3 = f32[8,16,384]{2,1,0:T(8,128)S(1)} fusion(bf16[8,4,16,384]{3,2,1,0:T(8,128)(2,1)S(1)} %bitcast.139, bf16[8,4,384,384]{3,2,1,0:T(8,128)(2,1)} %param.13), kind=kOutput, calls=%fused_computation.9 | convolution fusion | flops 150994944 | bytes 10027008 | tf_op jit(solution)/shard_map/pjvw,pjkw->pkv/dot_general | solution.py:59
  109.5 13.5 %psum.31 = f32[16,16]{1,0:T(8,128)S(1)} all-reduce(f32[16,16]{1,0:T(8,128)S(1)} %convolution_bitcast_fusion.12), channel_id=1, replica_groups=mesh['patch'=8,'rhs'=4] {'patch'}, use_global_device_ids=true, to_apply=%region_5.8 | all-reduce | flops 256 | bytes 2048 | tf_op jit(solution)/shard_map/psum | solution.py:107
  123.1 1.5 %cholesky.81 = f32[16,16]{1,0:T(8,128)S(1)} custom-call(f32[16,16]{1,0:T(8,128)S(1)} %fusion.26), custom_call_target="Cholesky" | custom-call | tf_op jit(solution)/shard_map/jit(cholesky)/cholesky | solution.py:25
  125.9 1.2 custom-call.11
  (68 shorter events, 13.9 us)
Async XLA Ops:
  0.6 41.6 %copy-start = (f32[8,384,64]{1,2,0:T(8,128)S(1)}, f32[8,384,64]{1,2,0:T(8,128)}, u32[]{:S(2)}) copy-start(f32[8,384,64]{1,2,0:T(8,128)} %param.20) | copy-start | bytes 2359300
  17.0 18.1 %collective-permute-start.1 = (bf16[8,16,384]{2,1,0:T(8,128)(2,1)S(1)}, bf16[8,16,384]{2,1,0:T(8,128)(2,1)S(1)}, u32[]{:S(2)}, u32[]{:S(2)}) collective-permute-start(bf16[8,16,384]{2,1,0:T(8,128)(2,1)S(1)} %copy.116), channel_id=1, source_target_pairs={{4,0},{8,4},{12,8},{16,12},{20,16},{24,20},{28,24},{0,28},{5,1},{9... | collective-permute-start | bytes 294920 | tf_op jit(solution)/shard_map/ppermute | solution.py:19
  17.1 18.1 %collective-permute-start = (bf16[8,16,384]{2,1,0:T(8,128)(2,1)S(1)}, bf16[8,16,384]{2,1,0:T(8,128)(2,1)S(1)}, u32[]{:S(2)}, u32[]{:S(2)}) collective-permute-start(bf16[8,16,384]{2,1,0:T(8,128)(2,1)S(1)} %copy.116), channel_id=1, source_target_pairs={{0,4},{4,8},{8,12},{12,16},{16,20},{20,24},{24,28},{28,0},{1,5},{5... | collective-permute-start | bytes 294920 | tf_op jit(solution)/shard_map/ppermute | solution.py:16
  35.8 54.0 %copy-start.1 = (f32[8,64,384]{2,1,0:T(8,128)S(1)}, f32[8,64,384]{2,1,0:T(8,128)}, u32[]{:S(2)}) copy-start(f32[8,64,384]{2,1,0:T(8,128)} %param.15) | copy-start | bytes 2359300
  35.9 54.9 %copy-start.2 = (f32[8,64,64]{2,1,0:T(8,128)S(1)}, f32[8,64,64]{2,1,0:T(8,128)}, u32[]{:S(2)}) copy-start(f32[8,64,64]{2,1,0:T(8,128)} %param.16) | copy-start | bytes 393220
  35.9 64.6 %copy-start.5 = (s32[1,4]{1,0:T(1,128)S(1)}, s32[1,4]{1,0:T(1,128)}, u32[]{:S(2)}) copy-start(s32[1,4]{1,0:T(1,128)} %param.17) | copy-start | bytes 52
  35.9 64.8 %copy-start.4 = (f32[1,4,64,64]{3,2,1,0:T(8,128)S(1)}, f32[1,4,64,64]{3,2,1,0:T(8,128)}, u32[]{:S(2)}) copy-start(f32[1,4,64,64]{3,2,1,0:T(8,128)} %param.18) | copy-start | bytes 196612
  35.9 65.0 %copy-start.3 = (f32[8,64,64]{2,1,0:T(8,128)S(1)}, f32[8,64,64]{2,1,0:T(8,128)}, u32[]{:S(2)}) copy-start(f32[8,64,64]{2,1,0:T(8,128)} %param.19) | copy-start | bytes 393220
  89.0 12.6 %collective-permute-start.3 = (bf16[8,16,384]{2,1,0:T(8,128)(2,1)S(1)}, bf16[8,16,384]{2,1,0:T(8,128)(2,1)S(1)}, u32[]{:S(2)}, u32[]{:S(2)}) collective-permute-start(bf16[8,16,384]{2,1,0:T(8,128)(2,1)S(1)} %get-tuple-element.6), channel_id=1, source_target_pairs={{4,0},{8,4},{12,8},{16,12},{20,16},{24,20},{28,24},{0,28},{5,1},{9... | collective-permute-start | bytes 294920 | tf_op jit(solution)/shard_map/ppermute | solution.py:19
  89.0 12.6 %collective-permute-start.2 = (bf16[8,16,384]{2,1,0:T(8,128)(2,1)S(1)}, bf16[8,16,384]{2,1,0:T(8,128)(2,1)S(1)}, u32[]{:S(2)}, u32[]{:S(2)}) collective-permute-start(bf16[8,16,384]{2,1,0:T(8,128)(2,1)S(1)} %get-tuple-element.6), channel_id=1, source_target_pairs={{0,4},{4,8},{8,12},{12,16},{16,20},{20,24},{24,28},{28,0},{1,5},{5... | collective-permute-start | bytes 294920 | tf_op jit(solution)/shard_map/ppermute | solution.py:16
where the time goes:
time: 130 us; the launch traced here: 129 us
  blocking collectives  83.3 us (64%)
  matrix products  27.2 us (21%)
  other arithmetic  14.2 us (11%)
  local copies, waits for them, and re-layouts  2.76 us (2%)
    psum x2, blocking collectives, residual_sum(): return lax.psum(gram(residual, residual), 'patch')  35.7 us
    all_gather x2, blocking collectives, apply_operator(): piece = lax.all_gather(cell_moment[None], 'patch', axis=0, tiled=True)  18.7 us
    all_gather x1, blocking collectives, on_device(): residual = lax.all_gather(rhs_vectors, 'rhs', axis=1, tiled=True)  15.5 us
    psum x1, blocking collectives, on_device(): curve = lax.psum(gram(direction, image), 'patch')  13.5 us
    dot_general x2, matrix products, apply_operator(): jnp.einsum('pjvw,pjkw->pkv', near_blocks, picked, preferred_element_type=...  12.5 us
    another operation x9, other arithmetic, spd_solve(): factor = jnp.linalg.cholesky(matrix)  6.39 us
    another operation x6, other arithmetic, spd_solve(): return jax.scipy.linalg.cho_solve((factor, True), right)  5.63 us
    dot_general x2, matrix products, apply_operator(): moments = jnp.einsum('pew,pkw->pke', up_maps, field, precision=HIGH)  2.99 us
  transfers between devices with their start and end apart: 4, of which 0 were waited for; matrix products, arithmetic and copies ran while one was open for 8% of the time, Pallas kernels for 0%

commit v1 on v0

--- a/solution.py
+++ b/solution.py
@@ -86,7 +86,12 @@
 ):
     my_cols = rhs_vectors.shape[1]
     offset = lax.axis_index("rhs") * my_cols
-    residual = lax.all_gather(rhs_vectors, "rhs", axis=1, tiled=True)
+    ring = [rhs_vectors]
+    for hop in range(3):
+        ring.append(lax.ppermute(ring[-1], "rhs", [(dev, (dev + 1) % 4) for dev in range(4)]))
+    residual = jnp.roll(
+        jnp.concatenate(ring[::-1], axis=1), (lax.axis_index("rhs") + 1) * ring[0].shape[1], axis=1
+    )
     solution = jnp.zeros_like(residual)
     direction = residual
     current = jnp.zeros((residual.shape[1], residual.shape[1]), jnp.float32)

time: 130 us -> 134 us (1.031)
  blocking collectives: 83.3 us -> 68 us
  waiting for transfers between devices: 0.03 us -> 15.2 us
  starting transfers between devices: 1.11 us -> 4.22 us
    all_gather x1 -> x0, blocking collectives: 15.5 us -> none  [on_device(): residual = lax.all_gather(rhs_vectors, 'rhs', axis=1, tiled=True)]
    ppermute x0 -> x3, waiting for transfers between devices: none -> 15.2 us  [on_device(): lax.ppermute(ring[-1], 'rhs', [(dev, (dev + 1) % 4) for dev in range(4)])]
    ppermute x0 -> x3, starting transfers between devices: none -> 3.11 us  [on_device(): lax.ppermute(ring[-1], 'rhs', [(dev, (dev + 1) % 4) for dev in range(4)])]
    concatenate x0 -> x1, local copies, waits for them, and re-layouts: none -> 1.79 us  [on_device(): jnp.roll(jnp.concatenate(ring[::-1], axis=1), (lax.axis_index('rhs') + 1)...]
  transfers between devices with their start and end apart: 4 -> 7, of which waited for: 0 -> 3; matrix products, arithmetic and copies ran while one was open for 8% -> 8% of each run, Pallas kernels for 0% -> 0%
where the time goes in v1:
time: 134 us; the launch traced here: 133 us
  blocking collectives  68 us (51%)
  matrix products  27.3 us (20%)
  waiting for transfers between devices  15.2 us (11%)
  other arithmetic  14.1 us (11%)
  starting transfers between devices  4.22 us (3%)
  local copies, waits for them, and re-layouts  3.67 us (3%)
    psum x2, blocking collectives, residual_sum(): return lax.psum(gram(residual, residual), 'patch')  35.7 us
    all_gather x2, blocking collectives, apply_operator(): piece = lax.all_gather(cell_moment[None], 'patch', axis=0, tiled=True)  18.9 us
    ppermute x3, waiting for transfers between devices, on_device(): lax.ppermute(ring[-1], 'rhs', [(dev, (dev + 1) % 4) for dev in range(4)])  15.2 us
    psum x1, blocking collectives, on_device(): curve = lax.psum(gram(direction, image), 'patch')  13.5 us
    dot_general x2, matrix products, apply_operator(): jnp.einsum('pjvw,pjkw->pkv', near_blocks, picked, preferred_element_type=...  12.5 us
    another operation x9, other arithmetic, spd_solve(): factor = jnp.linalg.cholesky(matrix)  6.39 us
    another operation x6, other arithmetic, spd_solve(): return jax.scipy.linalg.cho_solve((factor, True), right)  5.63 us
    ppermute x3, starting transfers between devices, on_device(): lax.ppermute(ring[-1], 'rhs', [(dev, (dev + 1) % 4) for dev in range(4)])  3.11 us
  transfers between devices with their start and end apart: 7, of which 3 were waited for; matrix products, arithmetic and copies ran while one was open for 8% of the time, Pallas kernels for 0%

profile of v1, /device:TPU:0, one launch (start us, length us, event | category | flops | bytes accessed | tf_op | source)
XLA Modules:
  0.0 133.5 jit_solution(12043652488064796350)
XLA Ops:
  0.6 3.1 %collective-permute-start = (f32[8,4,384]{2,1,0:T(4,128)}, f32[8,4,384]{2,1,0:T(4,128)S(1)}, u32[]{:S(2)}, u32[]{:S(2)}) collective-permute-start(f32[8,4,384]{2,1,0:T(4,128)} %param.12), channel_id=1, source_target_pairs={{0,1},{1,2},{2,3},{3,0},{4,5},{5,6},{6,7},{7,4},{8,9},{9,10},{10,1... | collective-permute-start | bytes 147464 | tf_op jit(solution)/shard_map/ppermute | solution.py:91
  3.8 4.3 %collective-permute-done = f32[8,4,384]{2,1,0:T(4,128)S(1)} collective-permute-done((f32[8,4,384]{2,1,0:T(4,128)}, f32[8,4,384]{2,1,0:T(4,128)S(1)}, u32[]{:S(2)}, u32[]{:S(2)}) %collective-permute-start) | collective-permute-done | bytes 49184 | tf_op jit(solution)/shard_map/ppermute | solution.py:91
  8.9 5.0 %collective-permute-done.1 = f32[8,4,384]{2,1,0:T(4,128)S(1)} collective-permute-done((f32[8,4,384]{2,1,0:T(4,128)S(1)}, f32[8,4,384]{2,1,0:T(4,128)S(1)}, u32[]{:S(2)}, u32[]{:S(2)}) %collective-permute-start.1) | collective-permute-done | bytes 49184 | tf_op jit(solution)/shard_map/ppermute | solution.py:91
  14.0 5.9 %collective-permute-done.2 = f32[8,4,384]{2,1,0:T(4,128)S(1)} collective-permute-done((f32[8,4,384]{2,1,0:T(4,128)S(1)}, f32[8,4,384]{2,1,0:T(4,128)S(1)}, u32[]{:S(2)}, u32[]{:S(2)}) %collective-permute-start.2) | collective-permute-done | bytes 49184 | tf_op jit(solution)/shard_map/ppermute | solution.py:91
  19.8 1.8 %concatenate.12 = f32[8,32,384]{2,1,0:T(8,128)S(1)} concatenate(f32[8,4,384]{2,1,0:T(4,128)S(1)} %collective-permute-done.2, f32[8,4,384]{2,1,0:T(4,128)S(1)} %collective-permute-done.1, f32[8,4,384]{2,1,0:T(4,128)S(1)} %collective-permute-done, f32[8,4,384]{2,1,0:T(4,128)} %param.12, f32[8,4,384]{2,1,0:T(4,128)S(1)} %collective-permute-done.2, ...), dimensions={1} | concatenate | bytes 786432 | tf_op jit(solution)/shard_map/jit(_roll_dynamic)/concatenate | solution.py:92
  22.2 2.1 %fusion.11 = f32[8,16,64]{2,1,0:T(8,128)S(1)} fusion(f32[8,64,384]{2,1,0:T(8,128)} %param.15, f32[8,32,384]{2,1,0:T(8,128)S(1)} %concatenate.12, s32[]{:T(128)S(6)} %select_n.33), kind=kOutput, calls=%fused_computation.33 | convolution fusion | flops 37748736 | bytes 1015812 | tf_op jit(solution)/shard_map/pew,pkw->pke/dot_general | solution.py:60
  24.3 1.2 convolution_bitcast_fusion.11
  25.5 9.5 %all-gather = f32[128,64]{1,0:T(8,128)S(1)} all-gather(f32[16,64]{1,0:T(8,128)S(1)} %convolution_bitcast_fusion.11), channel_id=2, replica_groups=mesh['patch'=8,'rhs'=4] {'patch'}, dimensions={0}, use_global_device_ids=true | all-gather | bytes 36864 | tf_op jit(solution)/shard_map/all_gather | solution.py:64
  35.0 0.9 fusion.15
  35.9 1.1 fusion.4
  37.0 1.7 %convolution_bitcast_fusion.6 = f32[8,16,64]{2,1,0:T(8,128)S(1)} fusion(f32[16,64,1]{1,0,2:T(8,128)S(1)} %fusion.4, f32[8,64,64]{2,1,0:T(8,128)} %param.19), kind=kOutput, calls=%fused_computation.12 | convolution fusion | flops 6291456 | bytes 167936 | tf_op jit(solution)/shard_map/pfe,ke->pkf/dot_general | solution.py:71
  39.9 6.3 %convolution_bitcast_fusion.4 = f32[8,16,384]{2,1,0:T(8,128)S(1)} fusion(bf16[8,4,16,384]{3,2,1,0:T(8,128)(2,1)S(1)} %bitcast.138, bf16[8,4,384,384]{3,2,1,0:T(8,128)(2,1)} %param.13), kind=kOutput, calls=%fused_computation.10 | convolution fusion | flops 150994944 | bytes 10027008 | tf_op jit(solution)/shard_map/pjvw,pjkw->pkv/dot_general | solution.py:59
  47.2 23.6 %all-reduce = (f32[16,16]{0,1:T(8,128)S(1)}, f32[16,16]{1,0:T(8,128)S(1)}) all-reduce(f32[16,16]{0,1:T(8,128)S(1)} %convolution_bitcast_fusion.14, f32[16,16]{1,0:T(8,128)S(1)} %convolution_bitcast_fusion.15), channel_id=1, replica_groups=mesh['patch'=8,'rhs'=4] {'patch'}, use_global_device_ids=true, to_apply=%region_3.5 | all-reduce | flops 512 | bytes 4096 | tf_op jit(solution)/shard_map/psum | solution.py:38
  70.9 1.5 %cholesky.59 = f32[16,16]{1,0:T(8,128)S(1)} custom-call(f32[16,16]{1,0:T(8,128)S(1)} %fusion.35), custom_call_target="Cholesky" | custom-call | tf_op jit(solution)/shard_map/jit(cholesky)/cholesky | solution.py:25
  73.7 1.2 custom-call.9
  76.1 12.1 %psum.30 = f32[16,16]{1,0:T(8,128)S(1)} all-reduce(f32[16,16]{1,0:T(8,128)S(1)} %convolution_bitcast_fusion.13), channel_id=1, replica_groups=mesh['patch'=8,'rhs'=4] {'patch'}, use_global_device_ids=true, to_apply=%region_4.7 | all-reduce | flops 256 | bytes 2048 | tf_op jit(solution)/shard_map/psum | solution.py:38
  88.2 1.4 %cholesky.70 = f32[16,16]{1,0:T(8,128)S(1)} custom-call(f32[16,16]{1,0:T(8,128)S(1)} %fusion.31), custom_call_target="Cholesky" | custom-call | tf_op jit(solution)/shard_map/jit(cholesky)/cholesky | solution.py:25
  91.0 1.2 custom-call.10
  93.5 0.9 fusion.49
  94.7 9.4 %all-gather.1 = f32[128,64]{1,0:T(8,128)S(1)} all-gather(f32[16,64]{1,0:T(8,128)S(1)} %convolution_bitcast_fusion.8), channel_id=3, replica_groups=mesh['patch'=8,'rhs'=4] {'patch'}, dimensions={0}, use_global_device_ids=true | all-gather | bytes 36864 | tf_op jit(solution)/shard_map/all_gather | solution.py:64
  106.3 6.2 %convolution_bitcast_fusion.3 = f32[8,16,384]{2,1,0:T(8,128)S(1)} fusion(bf16[8,4,16,384]{3,2,1,0:T(8,128)(2,1)S(1)} %bitcast.137, bf16[8,4,384,384]{3,2,1,0:T(8,128)(2,1)} %param.13), kind=kOutput, calls=%fused_computation.9 | convolution fusion | flops 150994944 | bytes 10027008 | tf_op jit(solution)/shard_map/pjvw,pjkw->pkv/dot_general | solution.py:59
  113.5 13.5 %psum.31 = f32[16,16]{1,0:T(8,128)S(1)} all-reduce(f32[16,16]{1,0:T(8,128)S(1)} %convolution_bitcast_fusion.12), channel_id=1, replica_groups=mesh['patch'=8,'rhs'=4] {'patch'}, use_global_device_ids=true, to_apply=%region_5.8 | all-reduce | flops 256 | bytes 2048 | tf_op jit(solution)/shard_map/psum | solution.py:112
  127.1 1.5 %cholesky.81 = f32[16,16]{1,0:T(8,128)S(1)} custom-call(f32[16,16]{1,0:T(8,128)S(1)} %fusion.26), custom_call_target="Cholesky" | custom-call | tf_op jit(solution)/shard_map/jit(cholesky)/cholesky | solution.py:25
  129.9 1.2 custom-call.11
  (73 shorter events, 16.0 us)
Async XLA Ops:
  0.6 45.6 %copy-start = (f32[8,384,64]{1,2,0:T(8,128)S(1)}, f32[8,384,64]{1,2,0:T(8,128)}, u32[]{:S(2)}) copy-start(f32[8,384,64]{1,2,0:T(8,128)} %param.20) | copy-start | bytes 2359300
  0.6 7.4 %collective-permute-start = (f32[8,4,384]{2,1,0:T(4,128)}, f32[8,4,384]{2,1,0:T(4,128)S(1)}, u32[]{:S(2)}, u32[]{:S(2)}) collective-permute-start(f32[8,4,384]{2,1,0:T(4,128)} %param.12), channel_id=1, source_target_pairs={{0,1},{1,2},{2,3},{3,0},{4,5},{5,6},{6,7},{7,4},{8,9},{9,10},{10,1... | collective-permute-start | bytes 147464 | tf_op jit(solution)/shard_map/ppermute | solution.py:91
  8.1 5.9 %collective-permute-start.1 = (f32[8,4,384]{2,1,0:T(4,128)S(1)}, f32[8,4,384]{2,1,0:T(4,128)S(1)}, u32[]{:S(2)}, u32[]{:S(2)}) collective-permute-start(f32[8,4,384]{2,1,0:T(4,128)S(1)} %collective-permute-done), channel_id=1, source_target_pairs={{0,1},{1,2},{2,3},{3,0},{4,5},{5,6},{6,7},{7,4},{8,9},{9,10},{10,1... | collective-permute-start | bytes 147464 | tf_op jit(solution)/shard_map/ppermute | solution.py:91
  13.9 5.9 %collective-permute-start.2 = (f32[8,4,384]{2,1,0:T(4,128)S(1)}, f32[8,4,384]{2,1,0:T(4,128)S(1)}, u32[]{:S(2)}, u32[]{:S(2)}) collective-permute-start(f32[8,4,384]{2,1,0:T(4,128)S(1)} %collective-permute-done.1), channel_id=1, source_target_pairs={{0,1},{1,2},{2,3},{3,0},{4,5},{5,6},{6,7},{7,4},{8,9},{9,10},{10,1... | collective-permute-start | bytes 147464 | tf_op jit(solution)/shard_map/ppermute | solution.py:91
  21.7 17.4 %collective-permute-start.4 = (bf16[8,16,384]{2,1,0:T(8,128)(2,1)S(1)}, bf16[8,16,384]{2,1,0:T(8,128)(2,1)S(1)}, u32[]{:S(2)}, u32[]{:S(2)}) collective-permute-start(bf16[8,16,384]{2,1,0:T(8,128)(2,1)S(1)} %dynamic-slice_convert_fusion), channel_id=1, source_target_pairs={{4,0},{8,4},{12,8},{16,12},{20,16},{24,20},{28,24},{0,28},{5,1},{9... | collective-permute-start | bytes 294920 | tf_op jit(solution)/shard_map/ppermute | solution.py:19
  21.7 17.4 %collective-permute-start.3 = (bf16[8,16,384]{2,1,0:T(8,128)(2,1)S(1)}, bf16[8,16,384]{2,1,0:T(8,128)(2,1)S(1)}, u32[]{:S(2)}, u32[]{:S(2)}) collective-permute-start(bf16[8,16,384]{2,1,0:T(8,128)(2,1)S(1)} %dynamic-slice_convert_fusion), channel_id=1, source_target_pairs={{0,4},{4,8},{8,12},{12,16},{16,20},{20,24},{24,28},{28,0},{1,5},{5... | collective-permute-start | bytes 294920 | tf_op jit(solution)/shard_map/ppermute | solution.py:16
  39.8 53.7 %copy-start.1 = (f32[8,64,384]{2,1,0:T(8,128)S(1)}, f32[8,64,384]{2,1,0:T(8,128)}, u32[]{:S(2)}) copy-start(f32[8,64,384]{2,1,0:T(8,128)} %param.15) | copy-start | bytes 2359300
  39.8 54.6 %copy-start.2 = (f32[8,64,64]{2,1,0:T(8,128)S(1)}, f32[8,64,64]{2,1,0:T(8,128)}, u32[]{:S(2)}) copy-start(f32[8,64,64]{2,1,0:T(8,128)} %param.16) | copy-start | bytes 393220
  39.8 64.2 %copy-start.5 = (s32[1,4]{1,0:T(1,128)S(1)}, s32[1,4]{1,0:T(1,128)}, u32[]{:S(2)}) copy-start(s32[1,4]{1,0:T(1,128)} %param.17) | copy-start | bytes 52
  39.8 64.4 %copy-start.4 = (f32[1,4,64,64]{3,2,1,0:T(8,128)S(1)}, f32[1,4,64,64]{3,2,1,0:T(8,128)}, u32[]{:S(2)}) copy-start(f32[1,4,64,64]{3,2,1,0:T(8,128)} %param.18) | copy-start | bytes 196612
  39.9 64.6 %copy-start.3 = (f32[8,64,64]{2,1,0:T(8,128)S(1)}, f32[8,64,64]{2,1,0:T(8,128)}, u32[]{:S(2)}) copy-start(f32[8,64,64]{2,1,0:T(8,128)} %param.19) | copy-start | bytes 393220
  92.9 12.6 %collective-permute-start.6 = (bf16[8,16,384]{2,1,0:T(8,128)(2,1)S(1)}, bf16[8,16,384]{2,1,0:T(8,128)(2,1)S(1)}, u32[]{:S(2)}, u32[]{:S(2)}) collective-permute-start(bf16[8,16,384]{2,1,0:T(8,128)(2,1)S(1)} %get-tuple-element.6), channel_id=1, source_target_pairs={{4,0},{8,4},{12,8},{16,12},{20,16},{24,20},{28,24},{0,28},{5,1},{9... | collective-permute-start | bytes 294920 | tf_op jit(solution)/shard_map/ppermute | solution.py:19
  93.0 12.6 %collective-permute-start.5 = (bf16[8,16,384]{2,1,0:T(8,128)(2,1)S(1)}, bf16[8,16,384]{2,1,0:T(8,128)(2,1)S(1)}, u32[]{:S(2)}, u32[]{:S(2)}) collective-permute-start(bf16[8,16,384]{2,1,0:T(8,128)(2,1)S(1)} %get-tuple-element.6), channel_id=1, source_target_pairs={{0,4},{4,8},{8,12},{12,16},{16,20},{20,24},{24,28},{28,0},{1,5},{5... | collective-permute-start | bytes 294920 | tf_op jit(solution)/shard_map/ppermute | solution.py:16
